TPU v7x, 16 devices: a whole 2x2x2 slice. The times are simulated.
16 devices in a mesh: dp: 2 (over z), ep: 8 (over y, x, core).
Axes of the slice: x: 2, y: 2, z: 2, core: 2. Of those that a mesh axis runs over, the one named last changes fastest.
Arguments:
- hidden: bfloat16 [4096, 1536], P(('dp', 'ep')), parts along dimension 0
- router_w: float32 [1536, 32], replicated
- expert_ids: int32 [4096, 2], P(('dp', 'ep')), parts along dimension 0
- w_gate: bfloat16 [32, 1536, 2304], P('ep')
- w_up: bfloat16 [32, 1536, 2304], P('ep')
- w_down: bfloat16 [32, 2304, 1536], P('ep')
- post_scale: float32 [2], replicated
Outputs:
- output: bfloat16 [4096, 1536], P(('dp', 'ep')), parts along dimension 0
There are 2 independent parts. A program takes and returns all parts, laid end to end along the dimension named above; an argument that names none is the same for every part.
All inputs are finite; a program needn't handle non-finite values.
Results may differ from a plain program's by a relative error of at most 0.001.
Values are sent between devices in bfloat16 or wider.
A program may use at most 1 GiB of HBM per device.

v0:
```python
import functools

import jax
import jax.numpy as jnp
from jax import lax
from jax.experimental import pallas as pl
from jax.experimental.pallas import tpu as pltpu
from jax.sharding import PartitionSpec as P

MESH = pl.DeviceIdType.MESH
BF16, F32, I32 = jnp.bfloat16, jnp.float32, jnp.int32
GROUP = 8
LOCAL = 4
EXPERTS = GROUP * LOCAL
TOK = 256
SLOTS = 64
WIDTH = 1536
FFN = 2304
CHUNKS = 4
BASE = 16
EXTRA = SLOTS - BASE
BROWS = GROUP * BASE
BUCKETS = tuple(EXTRA * (i + 1) for i in range(LOCAL))
FCH = 768
NCH = FFN // FCH
DCH = 512
RING = 3
XROWS = GROUP * EXTRA + 128
GATHER_VMEM = 15
EXPERT_VMEM = 24
BASE_VMEM = 27


def dot(a, b):
    return jnp.dot(a, b, preferred_element_type=F32)


def dot_t(a, b):
    return lax.dot_general(a, b, (((1,), (1,)), ((), ())), preferred_element_type=F32)


def extra_rows(count):
    over = jnp.maximum(count - BASE, 0.0)
    return jnp.floor((over + 15.0) * (1.0 / 16.0)) * 16.0


def gather_kernel(ids_hbm, h_hbm, wr_hbm, xb_ref, xe_ref, cnt_ref, tab_ref, top_ref,
                  ids_ref, h_ref, wr_ref, in_sem, hall, rk, idbuf, needs, id_send, id_recv, x_send, y_send, p_send, x_recv, y_recv, d_recv, p_recv, own_sem):
    dp, me = lax.axis_index("dp"), lax.axis_index("ep")
    core, xc, yc = lax.rem(me, 2), lax.rem(me // 2, 2), me // 4
    xn, yn, pc = me + 2 - 4 * xc, me + 4 - 8 * yc, me + 1 - 2 * core
    dg = xn + 4 - 8 * yc
    rows = TOK // CHUNKS
    inputs = [pltpu.make_async_copy(src, dst, in_sem.at[i]) for i, (src, dst) in enumerate([(ids_hbm, ids_ref), (h_hbm, h_ref), (wr_hbm, wr_ref)])]
    for copy in inputs:
        copy.start()

    barrier = pltpu.get_barrier_semaphore()
    for k in range(1, GROUP):
        pl.semaphore_signal(barrier, inc=1, device_id={"ep": lax.rem(me + k, GROUP)}, device_id_type=MESH)
    pl.semaphore_signal(barrier, inc=1, device_id={"dp": 1 - dp, "ep": me}, device_id_type=MESH)
    pl.semaphore_wait(barrier, GROUP)

    def piece(block, q):
        return hall.at[block, pl.ds(q * rows, rows), :]

    def mine(q):
        return h_ref.at[pl.ds(q * rows, rows), :]

    def remote(src, dst, send, recv, dev):
        return pltpu.make_async_remote_copy(src_ref=src, dst_ref=dst, send_sem=send, recv_sem=recv,
                                            device_id={"ep": dev}, device_id_type=MESH)

    half = CHUNKS // 2
    sends = []

    def start(copy):
        copy.start()
        sends.append(copy)

    def send_x(q):
        start(remote(mine(q), piece(me, q), x_send.at[q], x_recv.at[q], xn))

    def send_y(q):
        start(remote(mine(q), piece(me, q), y_send.at[q], y_recv.at[q], yn))

    inputs[0].wait()
    id_copies = []
    for k in range(1, GROUP):
        id_copies.append(remote(ids_ref, idbuf.at[me], id_send.at[k], id_recv.at[k], lax.rem(me + k, GROUP)))
        id_copies[-1].start()
    inputs[1].wait()
    for i in range(CHUNKS):
        send_x(i)
        send_y((i + half) % CHUNKS)
    start(remote(h_ref, hall.at[me], p_send.at[3 * CHUNKS], p_recv.at[3 * CHUNKS], pc))
    own_ids = pltpu.make_async_copy(ids_ref, idbuf.at[me], own_sem.at[0])
    own_ids.start()

    upper = (lax.broadcasted_iota(I32, (TOK, TOK), 0) < lax.broadcasted_iota(I32, (TOK, TOK), 1)).astype(BF16)
    hb = h_ref[...]
    inputs[2].wait()
    wr = wr_ref[...]
    w_hi = wr.astype(BF16)
    rest = wr - w_hi.astype(F32)
    w_mid = rest.astype(BF16)
    w_lo = (rest - w_mid.astype(F32)).astype(BF16)
    logits = dot_t(w_hi, hb) + (dot_t(w_mid, hb) + dot_t(w_lo, hb))
    prob = jnp.exp(logits - jnp.max(logits, axis=0, keepdims=True))
    prob = prob / jnp.sum(prob, axis=0, keepdims=True)
    e_iota = lax.broadcasted_iota(I32, (EXPERTS, TOK), 0)
    id0, id1 = ids_ref[0:1, :], ids_ref[1:2, :]
    hit0, hit1 = e_iota == id0, e_iota == id1
    pick0 = jnp.sum(jnp.where(hit0, prob, 0.0), axis=0, keepdims=True)
    pick1 = jnp.sum(jnp.where(hit1, prob, 0.0), axis=0, keepdims=True)
    both = pick0 + pick1
    hits = jnp.where(hit0 | hit1, 1.0, 0.0)
    rank = dot(hits.astype(BF16), upper)
    er, ec = lax.broadcasted_iota(I32, (EXPERTS, EXPERTS), 0), lax.broadcasted_iota(I32, (EXPERTS, EXPERTS), 1)
    before = ((er // LOCAL == ec // LOCAL) & (ec < er)).astype(BF16)
    extra = extra_rows(jnp.sum(hits, axis=1, keepdims=True))
    start_e = dot(before, jnp.broadcast_to(extra, (EXPERTS, 128)).astype(BF16))[:, 0:1]
    local = (lax.broadcasted_iota(I32, (EXPERTS, 1), 0) % LOCAL).astype(F32)
    place_b = jnp.where(rank < BASE, local * BASE + rank, -1.0)
    place_e = jnp.where(rank < BASE, -1.0, start_e + rank - BASE)

    def at(hit, place):
        return jnp.sum(jnp.where(hit, place, 0.0), axis=0, keepdims=True)

    own0, own1 = (id0 // LOCAL).astype(F32), (id1 // LOCAL).astype(F32)
    fields = jnp.concatenate([own0, at(hit0, place_b), at(hit0, place_e), pick0 / both,
                              own1, at(hit1, place_b), at(hit1, place_e), pick1 / both, jnp.zeros((120, TOK), F32)], axis=0)
    tab_ref[...] = fields.T

    own_ids.wait()
    for copy in id_copies:
        copy.wait()
    j_iota = lax.broadcasted_iota(I32, (8, TOK), 0)
    local_id = jnp.where(j_iota < LOCAL, me * LOCAL + j_iota, -1)
    hit_list = []
    for s in range(GROUP):
        pair = idbuf[s]
        hit_list.append((local_id == pair[0:1, :]) | (local_id == pair[1:2, :]))
    hit_f = jnp.where(jnp.concatenate(hit_list, axis=0), 1.0, 0.0)
    hit_b = hit_f.astype(BF16)
    rk[...] = jnp.where(hit_f > 0.5, dot(hit_b, upper), -1.0).astype(I32).reshape(GROUP, 8, TOK)
    cnt_ref[...] = dot_t(jnp.ones((8, TOK), BF16), hit_b).astype(I32)
    lane = lax.broadcasted_iota(I32, (EXPERTS, 128), 1)
    spread = jnp.zeros((EXPERTS, 128), F32)
    for g in range(GROUP):
        pair = idbuf[g]
        n = jnp.where((e_iota == pair[0:1, :]) | (e_iota == pair[1:2, :]), 1.0, 0.0)
        spread = jnp.where(lane == g, extra_rows(jnp.sum(n, axis=1, keepdims=True)), spread)
    groups = (lax.broadcasted_iota(I32, (GROUP, EXPERTS), 0) == lax.broadcasted_iota(I32, (GROUP, EXPERTS), 1) // LOCAL).astype(BF16)
    need = dot(groups, spread.astype(BF16))
    need = jnp.max(jnp.max(need, axis=1, keepdims=True), axis=0, keepdims=True)
    needs[0] = jnp.broadcast_to(need, (8, 128))

    def arrived(block, q, sem):
        remote(piece(block, q), piece(block, q), x_send.at[0], sem, xn).wait_recv()

    for i in range(half):
        a, b = i, i + half
        arrived(xn, a, x_recv.at[a])
        start(remote(piece(xn, a), piece(xn, a), y_send.at[CHUNKS + i], d_recv.at[a], yn))
        start(remote(piece(xn, a), piece(xn, a), p_send.at[a], p_recv.at[a], pc))
        arrived(yn, b, y_recv.at[b])
        start(remote(piece(yn, b), piece(yn, b), x_send.at[CHUNKS + i], d_recv.at[b], xn))
        start(remote(piece(yn, b), piece(yn, b), p_send.at[CHUNKS + b], p_recv.at[CHUNKS + b], pc))
    other = pltpu.make_async_remote_copy(src_ref=needs.at[0], dst_ref=needs.at[1], send_sem=id_send.at[0], recv_sem=id_recv.at[0],
                                         device_id={"dp": 1 - dp, "ep": me}, device_id_type=MESH)
    other.start()

    b_iota = lax.broadcasted_iota(I32, (BASE, TOK), 0)
    x_iota = lax.broadcasted_iota(I32, (EXTRA, TOK), 0) + BASE

    def pick(s, block):
        ranks = rk[s]
        table = jnp.concatenate([(b_iota == ranks[j:j + 1, :]).astype(F32) for j in range(LOCAL)]
                                + [(x_iota == ranks[j:j + 1, :]).astype(F32) for j in range(LOCAL)], axis=0).astype(BF16)
        rows = dot(table, block).astype(BF16)
        for j in range(LOCAL):
            xb_ref[j, pl.ds(pl.multiple_of(s * BASE, BASE), BASE), :] = rows[j * BASE:(j + 1) * BASE]
        xe_ref[s] = rows[LOCAL * BASE:]

    pick(me, hb)
    remote(hall.at[pc], hall.at[pc], x_send.at[0], p_recv.at[3 * CHUNKS], pc).wait_recv()
    pick(pc, hall[pc])
    for i in range(half):
        a, b = i + half, i
        arrived(xn, a, x_recv.at[a])
        start(remote(piece(xn, a), piece(xn, a), p_send.at[a], p_recv.at[a], pc))
        arrived(yn, b, y_recv.at[b])
        start(remote(piece(yn, b), piece(yn, b), p_send.at[CHUNKS + b], p_recv.at[CHUNKS + b], pc))
    for i in range(half):
        for q in (i, i + half):
            arrived(dg, q, d_recv.at[q])
            start(remote(piece(dg, q), piece(dg, q), p_send.at[2 * CHUNKS + q], p_recv.at[2 * CHUNKS + q], pc))
        if i == 0:
            pick(xn, hall[xn])
            pick(yn, hall[yn])
    turn = 1 - 2 * core
    for q in range(CHUNKS):
        arrived(xn + turn, q, p_recv.at[q])
        arrived(yn + turn, q, p_recv.at[CHUNKS + q])
    pick(xn + turn, hall[xn + turn])
    pick(yn + turn, hall[yn + turn])
    pick(dg, hall[dg])
    for q in range(CHUNKS):
        arrived(dg + turn, q, p_recv.at[2 * CHUNKS + q])
    pick(dg + turn, hall[dg + turn])
    other.wait()
    both_need = jnp.maximum(needs[0], needs[1])
    top_ref[...] = sum((both_need > cap).astype(I32) for cap in BUCKETS[:-1])
    for copy in sends:
        copy.wait_send()


def gather(ids_t, hidden, wr_t):
    vmem = pl.BlockSpec(memory_space=pltpu.VMEM)
    dma = pltpu.SemaphoreType.DMA
    return pl.pallas_call(
        gather_kernel,
        name="gather_rows",
        out_shape=[
            jax.ShapeDtypeStruct((LOCAL, BROWS, WIDTH), BF16),
            jax.ShapeDtypeStruct((GROUP, LOCAL * EXTRA, WIDTH), BF16),
            jax.ShapeDtypeStruct((8, GROUP * 8), I32),
            jax.ShapeDtypeStruct((TOK, 128), F32),
            jax.ShapeDtypeStruct((8, 128), I32),
        ],
        in_specs=[pl.BlockSpec(memory_space=pltpu.HBM)] * 3,
        out_specs=[vmem] * 5,
        scratch_shapes=[
            pltpu.VMEM((2, TOK), I32),
            pltpu.VMEM((TOK, WIDTH), BF16),
            pltpu.VMEM((EXPERTS, WIDTH), F32),
            dma((3,)),
            pltpu.VMEM((GROUP, TOK, WIDTH), BF16),
            pltpu.VMEM((GROUP, 8, TOK), I32),
            pltpu.VMEM((GROUP, 2, TOK), I32),
            pltpu.VMEM((2, 8, 128), F32),
            dma((GROUP,)), dma((GROUP,)),
            dma((2 * CHUNKS,)), dma((2 * CHUNKS,)), dma((3 * CHUNKS + 1,)),
            dma((CHUNKS,)), dma((CHUNKS,)), dma((CHUNKS,)), dma((3 * CHUNKS + 1,)),
            dma((1,)),
        ],
        compiler_params=pltpu.CompilerParams(collective_id=1, has_side_effects=True, vmem_limit_bytes=GATHER_VMEM * 2**20),
        cost_estimate=pl.CostEstimate(flops=20 * 10**9, bytes_accessed=20 * 10**6, transcendentals=0),
    )(ids_t, hidden, wr_t)


def extra_kernel(cnt, xe_ref, w1, w3, w2, ye_ref, xbuf, mid, b3, b2, offs, act, tot, w3_sem, w2_sem):
    def tiles(s, j):
        return (jnp.maximum(cnt[0, s * 8 + j] - BASE, 0) + 15) // 16 * 16

    active = jnp.int32(0)
    for j in range(LOCAL):
        at = jnp.int32(0)
        for s in range(GROUP):
            offs[s, j] = at
            at = at + tiles(s, j)
        tot[j] = at
        act[active] = j
        active = active + (at > 0).astype(I32)
    chunks = active * NCH

    def up_copy(g):
        slot = lax.rem(g, RING)
        cols = pl.ds(pl.multiple_of(lax.rem(g, NCH) * FCH, FCH), FCH)
        return pltpu.make_async_copy(w3.at[act[g // NCH], :, cols], b3.at[slot], w3_sem.at[slot])

    def down_copy(g):
        slot = lax.rem(g, RING)
        cols = pl.ds(pl.multiple_of(lax.rem(g, NCH) * DCH, DCH), DCH)
        return pltpu.make_async_copy(w2.at[act[g // NCH], :, cols], b2.at[slot], w2_sem.at[slot])

    def fetch(copy, g):
        @pl.when(g < chunks)
        def _():
            copy(g).start()

    for g in range(RING):
        fetch(up_copy, g)
    for g in range(RING):
        fetch(down_copy, g)

    def compact(s, carry):
        for j in range(LOCAL):
            @pl.when(tot[j] > 0)
            def _():
                xbuf[j, pl.ds(pl.multiple_of(offs[s, j], 16), EXTRA), :] = xe_ref[s, j * EXTRA:(j + 1) * EXTRA, :]
        return carry

    lax.fori_loop(0, GROUP, compact, 0)
    ye_ref[...] = jnp.zeros_like(ye_ref)

    def expert(a, carry):
        j = act[a]
        total = tot[j]
        blocks = (total + 127) // 128
        xbuf[j, pl.ds(pl.multiple_of(total, 16), 128), :] = jnp.zeros((128, WIDTH), BF16)

        def over_rows(body):
            for n in range(1, 4):
                @pl.when(blocks == n)
                def _():
                    body(n * 128)

        def up_step(f, c):
            g = a * NCH + f
            slot = lax.rem(g, RING)
            up_copy(g).wait()

            def body(n):
                x = xbuf[j, :n, :]
                for p in range(FCH // 256):
                    cols = pl.ds(pl.multiple_of(f * FCH + p * 256, 256), 256)
                    up = dot(x, w1[j, :, cols])
                    lin = dot(x, b3[slot, :, p * 256:(p + 1) * 256])
                    mid[:n, cols] = (jax.nn.silu(up) * lin).astype(BF16)

            over_rows(body)
            fetch(up_copy, g + RING)
            return c

        def down_step(f, c):
            g = a * NCH + f
            slot = lax.rem(g, RING)
            down_copy(g).wait()

            def body(n):
                cols = pl.ds(pl.multiple_of(f * DCH, DCH), DCH)
                xbuf[j, :n, cols] = dot(mid[:n, :], b2[slot]).astype(BF16)

            over_rows(body)
            fetch(down_copy, g + RING)
            return c

        lax.fori_loop(0, NCH, up_step, 0)
        lax.fori_loop(0, NCH, down_step, 0)
        return carry

    lax.fori_loop(0, active, expert, 0)

    def pack(s, carry):
        at = jnp.int32(0)
        for j in range(LOCAL):
            n = tiles(s, j)

            @pl.when(n > 0)
            def _():
                ye_ref[s, pl.ds(pl.multiple_of(at, 16), EXTRA), :] = xbuf[j, pl.ds(pl.multiple_of(offs[s, j], 16), EXTRA), :]
            at = at + n
        return carry

    lax.fori_loop(0, GROUP, pack, 0)


def extra(cnt, xe, w1, w3, w2):
    hbm = pl.BlockSpec(memory_space=pl.ANY)
    vmem = pl.BlockSpec(memory_space=pltpu.VMEM)
    dma = pltpu.SemaphoreType.DMA
    return pl.pallas_call(
        extra_kernel,
        name="extra_rows",
        out_shape=jax.ShapeDtypeStruct((GROUP, LOCAL * EXTRA, WIDTH), BF16),
        in_specs=[pl.BlockSpec(memory_space=pltpu.SMEM), vmem, vmem, hbm, hbm],
        out_specs=vmem,
        input_output_aliases={1: 0},
        scratch_shapes=[
            pltpu.VMEM((LOCAL, XROWS, WIDTH), BF16),
            pltpu.VMEM((GROUP * EXTRA, FFN), BF16),
            pltpu.VMEM((RING, WIDTH, FCH), BF16),
            pltpu.VMEM((RING, FFN, DCH), BF16),
            pltpu.SMEM((GROUP, LOCAL), I32),
            pltpu.SMEM((LOCAL + 1,), I32),
            pltpu.SMEM((LOCAL,), I32),
            dma((RING,)), dma((RING,)),
        ],
        compiler_params=pltpu.CompilerParams(vmem_limit_bytes=EXPERT_VMEM * 2**20),
        cost_estimate=pl.CostEstimate(flops=8 * 10**9, bytes_accessed=30 * 10**6, transcendentals=0),
    )(cnt, xe, w1, w3, w2)


def base_kernel(cap, scale, tab_ref, h_ref, xb_ref, ye_ref, w1, w3, w2, out_ref,
                land_e, land_b, yb, mid, b3, b2, mix0, mix1, w3_sem, w2_sem, e_send, e_recv, b_send, b_recv):
    me = lax.axis_index("ep")

    def up_copy(j, f):
        return pltpu.make_async_copy(w3.at[j, :, pl.ds(f * FCH, FCH)], b3.at[f], w3_sem.at[f])

    def down_copy(j, f):
        return pltpu.make_async_copy(w2.at[j, :, pl.ds(f * DCH, DCH)], b2.at[f], w2_sem.at[f])

    for f in range(NCH):
        up_copy(0, f).start()
    for f in range(NCH):
        down_copy(0, f).start()

    barrier = pltpu.get_barrier_semaphore()
    for k in range(1, GROUP):
        pl.semaphore_signal(barrier, inc=1, device_id={"ep": lax.rem(me + k, GROUP)}, device_id_type=MESH)
    pl.semaphore_wait(barrier, GROUP - 1)

    def e_copy(k):
        to = lax.rem(me + k, GROUP)
        return pltpu.make_async_remote_copy(src_ref=ye_ref.at[to, pl.ds(0, cap), :], dst_ref=land_e.at[me], send_sem=e_send.at[k], recv_sem=e_recv.at[k],
                                            device_id={"ep": to}, device_id_type=MESH)

    def b_copy(j, k):
        to = lax.rem(me + k, GROUP)
        return pltpu.make_async_remote_copy(src_ref=yb.at[j, pl.ds(pl.multiple_of(to * BASE, BASE), BASE), :],
                                            dst_ref=land_b.at[me, pl.ds(pl.multiple_of(j * BASE, BASE), BASE), :],
                                            send_sem=b_send.at[j, k], recv_sem=b_recv.at[j, k],
                                            device_id={"ep": to}, device_id_type=MESH)

    for k in range(1, GROUP):
        e_copy(k).start()
    land_e[me] = ye_ref[me, :cap, :]

    def expert(j, carry):
        x = xb_ref[j]
        for f in range(NCH):
            up_copy(j, f).wait()
            for p in range(FCH // 256):
                cols = pl.ds(f * FCH + p * 256, 256)
                up = dot(x, w1[j, :, cols])
                lin = dot(x, b3[f, :, p * 256:(p + 1) * 256])
                mid[:, cols] = (jax.nn.silu(up) * lin).astype(BF16)

            @pl.when(j + 1 < LOCAL)
            def _():
                up_copy(j + 1, f).start()
        for f in range(NCH):
            down_copy(j, f).wait()
            yb[j, :, f * DCH:(f + 1) * DCH] = dot(mid[...], b2[f]).astype(BF16)

            @pl.when(j + 1 < LOCAL)
            def _():
                down_copy(j + 1, f).start()
        land_b[me, pl.ds(pl.multiple_of(j * BASE, BASE), BASE), :] = yb[j, pl.ds(pl.multiple_of(me * BASE, BASE), BASE), :]
        for k in range(1, GROUP):
            b_copy(j, k).start()
        return carry

    lax.fori_loop(0, LOCAL, expert, 0)

    def table(field, start, size):
        place = tab_ref[:, field:field + 1]
        inside = (place >= start) & (place < start + size)
        col = jnp.where(inside, tab_ref[:, field // 4 * 4:field // 4 * 4 + 1] * size + place - start, -1.0).astype(I32)
        return (col == lax.broadcasted_iota(I32, (TOK, GROUP * size), 1)).astype(F32).astype(BF16)

    for k in range(1, GROUP):
        e_copy(k).wait()
    far = land_e[...].reshape(GROUP * cap, WIDTH)
    mix0[...] = dot(table(2, 0, cap), far)
    mix1[...] = dot(table(6, 0, cap), far)
    early = (LOCAL - 1) * BASE
    for first, size in ((0, early), (early, BASE)):
        for j in range(first // BASE, (first + size) // BASE):
            for k in range(1, GROUP):
                b_copy(j, k).wait()
        near = land_b[:, first:first + size, :].reshape(GROUP * size, WIDTH)
        y0 = mix0[...] + dot(table(1, first, size), near)
        y1 = mix1[...] + dot(table(5, first, size), near)
        if first == 0:
            mix0[...] = y0
            mix1[...] = y1
    mixed = tab_ref[:, 3:4] * y0 + tab_ref[:, 7:8] * y1
    out_ref[...] = (scale[0] * h_ref[...].astype(F32) + scale[1] * mixed).astype(BF16)


def base(index, cap, scale, tab, hidden, xb, ye, w1, w3, w2):
    vmem = pl.BlockSpec(memory_space=pltpu.VMEM)
    hbm = pl.BlockSpec(memory_space=pl.ANY)
    dma = pltpu.SemaphoreType.DMA
    return pl.pallas_call(
        functools.partial(base_kernel, cap),
        name=f"base_rows_{cap}",
        out_shape=jax.ShapeDtypeStruct((TOK, WIDTH), BF16),
        in_specs=[pl.BlockSpec(memory_space=pltpu.SMEM)] + [vmem] * 5 + [hbm] * 2,
        out_specs=vmem,
        scratch_shapes=[
            pltpu.VMEM((GROUP, cap, WIDTH), BF16),
            pltpu.VMEM((GROUP, LOCAL * BASE, WIDTH), BF16),
            pltpu.VMEM((LOCAL, BROWS, WIDTH), BF16),
            pltpu.VMEM((BROWS, FFN), BF16),
            pltpu.VMEM((RING, WIDTH, FCH), BF16),
            pltpu.VMEM((RING, FFN, DCH), BF16),
            pltpu.VMEM((TOK, WIDTH), F32),
            pltpu.VMEM((TOK, WIDTH), F32),
            dma((RING,)), dma((RING,)),
            dma((GROUP,)), dma((GROUP,)), dma((LOCAL, GROUP)), dma((LOCAL, GROUP)),
        ],
        compiler_params=pltpu.CompilerParams(collective_id=2 + index, has_side_effects=True, vmem_limit_bytes=BASE_VMEM * 2**20),
    )(scale, tab, hidden, xb, ye, w1, w3, w2)


def solution(mesh):
    def local_step(hidden, router_w, expert_ids, w_gate, w_up, w_down, post_scale):
        xb, xe, cnt, tab, top = gather(expert_ids.T, hidden, router_w.T)
        ye = extra(cnt, xe, w_gate, w_up, w_down)
        branches = [functools.partial(base, i, cap) for i, cap in enumerate(BUCKETS)]
        return lax.switch(top[0, 0], branches, post_scale, tab, hidden, xb, ye, w_gate, w_up, w_down)

    tok_spec = P(("dp", "ep"))
    return jax.shard_map(local_step, mesh=mesh, in_specs=(tok_spec, P(), tok_spec, P("ep"), P("ep"), P("ep"), P()), out_specs=tok_spec, check_vma=False)
```

profile of v0, /device:TPU:0, one launch (start us, length us, event | category | flops | bytes accessed | tf_op | source)
XLA Modules:
  0.0 86.3 jit_solution(2373074731016630900)
XLA Ops:
  0.0 0.0 copy-start
  0.0 0.9 %copy-done = f32[1536,32]{0,1:T(8,128)S(1)} copy-done((f32[1536,32]{0,1:T(8,128)S(1)}, f32[1536,32]{0,1:T(8,128)}, u32[]{:S(2)}) %copy-start) | copy-done | bytes 196632
  0.9 0.0 copy-start.1
  0.9 0.7 copy-done.1
  1.6 0.0 copy-start.2
  1.6 33.5 %gather_rows.1 = (bf16[4,128,1536]{2,1,0:T(8,128)(2,1)S(1)}, bf16[8,192,1536]{2,1,0:T(8,128)(2,1)S(1)}, s32[8,64]{1,0:T(8,128)S(1)}, f32[256,128]{1,0:T(8,128)S(1)}, s32[8,128]{1,0:T(8,128)S(1)}) custom-call(s32[2,256]{1,0:T(2,128)S(1)} %bitcast.4, bf16[256,1536]{1,0:T(8,128)(2,1)} %h_hbm.1, f32[32,1536]{1,0:T(8,128)S(1)} %bitcast.3), custom_call_target="tpu_custom_call" | custom-call | flops 20000000000 | bytes 20000000 | tf_op jit(solution)/shard_map/gather_rows/pallas_call | solution.py:222
  35.1 0.5 slice.3
  36.2 0.0 copy-done.2
  36.3 0.0 copy-start.3
  36.3 0.0 copy-start.4
  36.3 12.7 %extra_rows.1 = bf16[8,192,1536]{2,1,0:T(8,128)(2,1)S(1)} custom-call(s32[8,64]{1,0:T(8,128)S(1)} %get-tuple-element.114.cnt, bf16[8,192,1536]{2,1,0:T(8,128)(2,1)S(1)} %get-tuple-element.115.xe_ref, bf16[4,1536,2304]{2,1,0:T(8,128)(2,1)S(1)} %copy-done.2, bf16[4,1536,2304]{2,1,0:T(8,128)(2,1)} %w3.1, ...), custom_call_target="tpu_custom_call", output_to_operand_aliasing={{}: (1, {})} | custom-call | flops 8000000000 | bytes 30000000 | tf_op jit(solution)/shard_map/extra_rows/pallas_call | solution.py:364
  49.0 0.0 copy-done.3
  49.0 0.0 copy-done.4
  49.0 36.4 %conditional.1 = (bf16[256,1536]{1,0:T(8,128)(2,1)S(1)}) conditional(s32[]{:T(128)} %bitcast.2, (f32[2]{0:T(128)S(1)}, f32[256,128]{1,0:T(8,128)S(1)}, bf16[256,1536]{1,0:T(8,128)(2,1)S(1)}, bf16[4,128,1536]{2,1,0:T(8,128)(2,1)S(1)}, bf16[8,192,1536]{2,1,0:T(8,128)(2,1)S(1)}, ...), branch_computations={%region_0.0_spmd, %region_1.0_spmd, %region_2.0_spmd, %region_3.0_... | conditional | bytes 8 | solution.py:506
  49.2 35.7 %base_rows_48.1 = bf16[256,1536]{1,0:T(8,128)(2,1)S(1)} custom-call(f32[2]{0:T(128)S(1)} %get-tuple-element.121.scale, f32[256,128]{1,0:T(8,128)S(1)} %get-tuple-element.74.tab_ref, bf16[256,1536]{1,0:T(8,128)(2,1)S(1)} %get-tuple-element.76.h_ref, bf16[4,128,1536]{2,1,0:T(8,128)(2,1)S(1)} %get-tuple-element.77.xb_ref, ...), custom_call_target="tpu_custom_call" | custom-call | tf_op jit(solution)/shard_map/cond/branch_0_fun/base_rows_48/pallas_call | solution.py:479
  85.4 0.9 %copy.23 = bf16[256,1536]{1,0:T(8,128)(2,1)} copy(bf16[256,1536]{1,0:T(8,128)(2,1)S(1)} %get-tuple-element.116) | data formatting | bytes 1572864
Async XLA Ops:
  0.0 0.9 %copy-start = (f32[1536,32]{0,1:T(8,128)S(1)}, f32[1536,32]{0,1:T(8,128)}, u32[]{:S(2)}) copy-start(f32[1536,32]{0,1:T(8,128)} %param.12) | copy-start | bytes 589828
  0.9 0.7 copy-start.1
  1.6 34.6 %copy-start.2 = (bf16[4,1536,2304]{2,1,0:T(8,128)(2,1)S(1)}, bf16[4,1536,2304]{2,1,0:T(8,128)(2,1)}, u32[]{:S(2)}) copy-start(bf16[4,1536,2304]{2,1,0:T(8,128)(2,1)} %w1.1) | copy-start | bytes 84934656
  36.3 12.7 %copy-start.3 = (bf16[256,1536]{1,0:T(8,128)(2,1)S(1)}, bf16[256,1536]{1,0:T(8,128)(2,1)}, u32[]{:S(2)}) copy-start(bf16[256,1536]{1,0:T(8,128)(2,1)} %h_hbm.1) | copy-start | bytes 2359300
  36.3 12.7 %copy-start.4 = (f32[2]{0:T(128)S(1)}, f32[2]{0:T(128)}, u32[]{:S(2)}) copy-start(f32[2]{0:T(128)} %param.17) | copy-start | bytes 28
where the time goes:
time: 86 us; the launch traced here: 86.3 us
  Pallas kernels  81.8 us (95%)
  local copies, waits for them, and re-layouts  3.02 us (4%)
    pallas_call x1, Pallas kernels, base(): pl.pallas_call(functools.partial(base_kernel, cap), name=f'base_rows_{cap...  35.7 us
    pallas_call x1, Pallas kernels, gather(): pl.pallas_call(gather_kernel, name='gather_rows', out_shape=[jax.ShapeDty...  33.5 us
    pallas_call x1, Pallas kernels, extra(): pl.pallas_call(extra_kernel, name='extra_rows', out_shape=jax.ShapeDtypeS...  12.7 us
    unnamed x11, local copies, waits for them, and re-layouts  2.51 us

commit v1 on v0

--- a/solution.py
+++ b/solution.py
@@ -26,6 +26,7 @@
 DCH = 512
 RING = 3
 XROWS = GROUP * EXTRA + 128
+FIELDS = 5
 GATHER_VMEM = 15
 EXPERT_VMEM = 24
 BASE_VMEM = 27
@@ -44,14 +45,14 @@
     return jnp.floor((over + 15.0) * (1.0 / 16.0)) * 16.0
 
 
-def gather_kernel(ids_hbm, h_hbm, wr_hbm, xb_ref, xe_ref, cnt_ref, tab_ref, top_ref,
-                  ids_ref, h_ref, wr_ref, in_sem, hall, rk, idbuf, needs, id_send, id_recv, x_send, y_send, p_send, x_recv, y_recv, d_recv, p_recv, own_sem):
+def gather_kernel(ids_hbm, h_hbm, xb_ref, xe_ref, cnt_ref, tab_ref, top_ref,
+                  ids_ref, h_ref, in_sem, hall, rk, idbuf, needs, id_send, id_recv, x_send, y_send, p_send, x_recv, y_recv, d_recv, p_recv, own_sem):
     dp, me = lax.axis_index("dp"), lax.axis_index("ep")
     core, xc, yc = lax.rem(me, 2), lax.rem(me // 2, 2), me // 4
     xn, yn, pc = me + 2 - 4 * xc, me + 4 - 8 * yc, me + 1 - 2 * core
     dg = xn + 4 - 8 * yc
     rows = TOK // CHUNKS
-    inputs = [pltpu.make_async_copy(src, dst, in_sem.at[i]) for i, (src, dst) in enumerate([(ids_hbm, ids_ref), (h_hbm, h_ref), (wr_hbm, wr_ref)])]
+    inputs = [pltpu.make_async_copy(src, dst, in_sem.at[i]) for i, (src, dst) in enumerate([(ids_hbm, ids_ref), (h_hbm, h_ref)])]
     for copy in inputs:
         copy.start()
 
@@ -99,44 +100,35 @@
 
     upper = (lax.broadcasted_iota(I32, (TOK, TOK), 0) < lax.broadcasted_iota(I32, (TOK, TOK), 1)).astype(BF16)
     hb = h_ref[...]
-    inputs[2].wait()
-    wr = wr_ref[...]
-    w_hi = wr.astype(BF16)
-    rest = wr - w_hi.astype(F32)
-    w_mid = rest.astype(BF16)
-    w_lo = (rest - w_mid.astype(F32)).astype(BF16)
-    logits = dot_t(w_hi, hb) + (dot_t(w_mid, hb) + dot_t(w_lo, hb))
-    prob = jnp.exp(logits - jnp.max(logits, axis=0, keepdims=True))
-    prob = prob / jnp.sum(prob, axis=0, keepdims=True)
     e_iota = lax.broadcasted_iota(I32, (EXPERTS, TOK), 0)
     id0, id1 = ids_ref[0:1, :], ids_ref[1:2, :]
     hit0, hit1 = e_iota == id0, e_iota == id1
-    pick0 = jnp.sum(jnp.where(hit0, prob, 0.0), axis=0, keepdims=True)
-    pick1 = jnp.sum(jnp.where(hit1, prob, 0.0), axis=0, keepdims=True)
-    both = pick0 + pick1
     hits = jnp.where(hit0 | hit1, 1.0, 0.0)
     rank = dot(hits.astype(BF16), upper)
     er, ec = lax.broadcasted_iota(I32, (EXPERTS, EXPERTS), 0), lax.broadcasted_iota(I32, (EXPERTS, EXPERTS), 1)
     before = ((er // LOCAL == ec // LOCAL) & (ec < er)).astype(BF16)
     extra = extra_rows(jnp.sum(hits, axis=1, keepdims=True))
-    start_e = dot(before, jnp.broadcast_to(extra, (EXPERTS, 128)).astype(BF16))[:, 0:1]
+    wide = jnp.broadcast_to(extra, (EXPERTS, 128)).astype(BF16)
+    start_e = dot(before, wide)[:, 0:1]
+    partner = (er // (2 * LOCAL) == ec // (2 * LOCAL)) & (er // LOCAL != ec // LOCAL)
+    partner_rows = dot(partner.astype(BF16), wide)[:, 0:1]
+    owner = lax.broadcasted_iota(I32, (EXPERTS, 1), 0) // LOCAL
     local = (lax.broadcasted_iota(I32, (EXPERTS, 1), 0) % LOCAL).astype(F32)
     place_b = jnp.where(rank < BASE, local * BASE + rank, -1.0)
     place_e = jnp.where(rank < BASE, -1.0, start_e + rank - BASE)
-
-    def at(hit, place):
-        return jnp.sum(jnp.where(hit, place, 0.0), axis=0, keepdims=True)
-
-    own0, own1 = (id0 // LOCAL).astype(F32), (id1 // LOCAL).astype(F32)
-    fields = jnp.concatenate([own0, at(hit0, place_b), at(hit0, place_e), pick0 / both,
-                              own1, at(hit1, place_b), at(hit1, place_e), pick1 / both, jnp.zeros((120, TOK), F32)], axis=0)
-    tab_ref[...] = fields.T
+    moved = place_e >= EXTRA
+    place_p = jnp.where(moved, jnp.minimum(partner_rows, EXTRA) + place_e - EXTRA, place_e)
+    own_p = jnp.where(moved, owner + 1 - 2 * (owner % 2), owner).astype(F32)
+    rows_of = []
+    for hit in (hit0, hit1):
+        rows_of += [jnp.sum(jnp.where(hit, v, 0.0), axis=0, keepdims=True) for v in (owner.astype(F32), place_b, place_e, own_p, place_p)]
+    tab_ref[...] = jnp.concatenate(rows_of + [jnp.zeros((128 - len(rows_of), TOK), F32)], axis=0).T
 
     own_ids.wait()
     for copy in id_copies:
         copy.wait()
     j_iota = lax.broadcasted_iota(I32, (8, TOK), 0)
-    local_id = jnp.where(j_iota < LOCAL, me * LOCAL + j_iota, -1)
+    local_id = jnp.where(j_iota < LOCAL, me * LOCAL + j_iota, (pc - 1) * LOCAL + j_iota)
     hit_list = []
     for s in range(GROUP):
         pair = idbuf[s]
@@ -151,10 +143,13 @@
         pair = idbuf[g]
         n = jnp.where((e_iota == pair[0:1, :]) | (e_iota == pair[1:2, :]), 1.0, 0.0)
         spread = jnp.where(lane == g, extra_rows(jnp.sum(n, axis=1, keepdims=True)), spread)
-    groups = (lax.broadcasted_iota(I32, (GROUP, EXPERTS), 0) == lax.broadcasted_iota(I32, (GROUP, EXPERTS), 1) // LOCAL).astype(BF16)
-    need = dot(groups, spread.astype(BF16))
-    need = jnp.max(jnp.max(need, axis=1, keepdims=True), axis=0, keepdims=True)
-    needs[0] = jnp.broadcast_to(need, (8, 128))
+    d_iota, o_iota = lax.broadcasted_iota(I32, (GROUP, EXPERTS), 0), lax.broadcasted_iota(I32, (GROUP, EXPERTS), 1) // LOCAL
+    spread = spread.astype(BF16)
+    need = dot((d_iota == o_iota).astype(BF16), spread)
+    near = dot((d_iota + 1 - 2 * (d_iota % 2) == o_iota).astype(BF16), spread)
+    pooled = jnp.maximum(need - EXTRA, 0.0) + jnp.minimum(near, EXTRA)
+    needs[0, 0] = jnp.broadcast_to(jnp.max(jnp.max(need, axis=1, keepdims=True), axis=0, keepdims=True), (8, 128))
+    needs[0, 1] = jnp.broadcast_to(jnp.max(jnp.max(pooled, axis=1, keepdims=True), axis=0, keepdims=True), (8, 128))
 
     def arrived(block, q, sem):
         remote(piece(block, q), piece(block, q), x_send.at[0], sem, xn).wait_recv()
@@ -210,13 +205,14 @@
         arrived(dg + turn, q, p_recv.at[2 * CHUNKS + q])
     pick(dg + turn, hall[dg + turn])
     other.wait()
-    both_need = jnp.maximum(needs[0], needs[1])
-    top_ref[...] = sum((both_need > cap).astype(I32) for cap in BUCKETS[:-1])
+    need, pooled = jnp.maximum(needs[0, 0], needs[1, 0]), jnp.maximum(needs[0, 1], needs[1, 1])
+    rest = sum((need > cap).astype(I32) for cap in BUCKETS[1:-1]) + 2
+    top_ref[...] = jnp.where(need <= EXTRA, 0, jnp.where((pooled <= EXTRA) & (need <= 2 * EXTRA), 1, rest))
     for copy in sends:
         copy.wait_send()
 
 
-def gather(ids_t, hidden, wr_t):
+def gather(ids_t, hidden):
     vmem = pl.BlockSpec(memory_space=pltpu.VMEM)
     dma = pltpu.SemaphoreType.DMA
     return pl.pallas_call(
@@ -229,17 +225,16 @@
             jax.ShapeDtypeStruct((TOK, 128), F32),
             jax.ShapeDtypeStruct((8, 128), I32),
         ],
-        in_specs=[pl.BlockSpec(memory_space=pltpu.HBM)] * 3,
+        in_specs=[pl.BlockSpec(memory_space=pltpu.HBM)] * 2,
         out_specs=[vmem] * 5,
         scratch_shapes=[
             pltpu.VMEM((2, TOK), I32),
             pltpu.VMEM((TOK, WIDTH), BF16),
-            pltpu.VMEM((EXPERTS, WIDTH), F32),
-            dma((3,)),
+            dma((2,)),
             pltpu.VMEM((GROUP, TOK, WIDTH), BF16),
             pltpu.VMEM((GROUP, 8, TOK), I32),
             pltpu.VMEM((GROUP, 2, TOK), I32),
-            pltpu.VMEM((2, 8, 128), F32),
+            pltpu.VMEM((2, 2, 8, 128), F32),
             dma((GROUP,)), dma((GROUP,)),
             dma((2 * CHUNKS,)), dma((2 * CHUNKS,)), dma((3 * CHUNKS + 1,)),
             dma((CHUNKS,)), dma((CHUNKS,)), dma((CHUNKS,)), dma((3 * CHUNKS + 1,)),
@@ -247,10 +242,10 @@
         ],
         compiler_params=pltpu.CompilerParams(collective_id=1, has_side_effects=True, vmem_limit_bytes=GATHER_VMEM * 2**20),
         cost_estimate=pl.CostEstimate(flops=20 * 10**9, bytes_accessed=20 * 10**6, transcendentals=0),
-    )(ids_t, hidden, wr_t)
-
-
-def extra_kernel(cnt, xe_ref, w1, w3, w2, ye_ref, xbuf, mid, b3, b2, offs, act, tot, w3_sem, w2_sem):
+    )(ids_t, hidden)
+
+
+def extra_kernel(cnt, xe_ref, w1, w3, w2, ye_ref, ov_ref, xbuf, mid, b3, b2, offs, act, tot, w3_sem, w2_sem):
     def tiles(s, j):
         return (jnp.maximum(cnt[0, s * 8 + j] - BASE, 0) + 15) // 16 * 16
 
@@ -294,6 +289,7 @@
 
     lax.fori_loop(0, GROUP, compact, 0)
     ye_ref[...] = jnp.zeros_like(ye_ref)
+    ov_ref[...] = jnp.zeros_like(ov_ref)
 
     def expert(a, carry):
         j = act[a]
@@ -352,6 +348,16 @@
             def _():
                 ye_ref[s, pl.ds(pl.multiple_of(at, 16), EXTRA), :] = xbuf[j, pl.ds(pl.multiple_of(offs[s, j], 16), EXTRA), :]
             at = at + n
+
+        @pl.when(at <= (LOCAL - 1) * EXTRA)
+        def _():
+            ye_ref[s, pl.ds(pl.multiple_of(at, 16), EXTRA), :] = jnp.zeros((EXTRA, WIDTH), BF16)
+
+        behind = jnp.minimum(sum(tiles(s, LOCAL + j) for j in range(LOCAL)), EXTRA)
+        for t in range(EXTRA // 16):
+            @pl.when((at > EXTRA + 16 * t) & (behind + 16 * t < EXTRA))
+            def _():
+                ov_ref[s, pl.ds(pl.multiple_of(behind + 16 * t, 16), 16), :] = ye_ref[s, EXTRA + 16 * t:EXTRA + 16 * (t + 1), :]
         return carry
 
     lax.fori_loop(0, GROUP, pack, 0)
@@ -364,9 +370,9 @@
     return pl.pallas_call(
         extra_kernel,
         name="extra_rows",
-        out_shape=jax.ShapeDtypeStruct((GROUP, LOCAL * EXTRA, WIDTH), BF16),
+        out_shape=[jax.ShapeDtypeStruct((GROUP, LOCAL * EXTRA, WIDTH), BF16), jax.ShapeDtypeStruct((GROUP, EXTRA, WIDTH), BF16)],
         in_specs=[pl.BlockSpec(memory_space=pltpu.SMEM), vmem, vmem, hbm, hbm],
-        out_specs=vmem,
+        out_specs=[vmem] * 2,
         input_output_aliases={1: 0},
         scratch_shapes=[
             pltpu.VMEM((LOCAL, XROWS, WIDTH), BF16),
@@ -383,15 +389,15 @@
     )(cnt, xe, w1, w3, w2)
 
 
-def base_kernel(cap, scale, tab_ref, h_ref, xb_ref, ye_ref, w1, w3, w2, out_ref,
-                land_e, land_b, yb, mid, b3, b2, mix0, mix1, w3_sem, w2_sem, e_send, e_recv, b_send, b_recv):
+def base_kernel(cap, pooled, scale, ids_ref, wr_ref, tab_ref, h_ref, xb_ref, ye_ref, ov_ref, w1, w3, w2, out_ref,
+                land_e, land_b, yb, mid, b3, b2, mix0, mix1, pool, w3_sem, w2_sem, e_send, e_recv, b_send, b_recv):
     me = lax.axis_index("ep")
 
     def up_copy(j, f):
-        return pltpu.make_async_copy(w3.at[j, :, pl.ds(f * FCH, FCH)], b3.at[f], w3_sem.at[f])
+        return pltpu.make_async_copy(w3.at[j, :, pl.ds(pl.multiple_of(f * FCH, FCH), FCH)], b3.at[f], w3_sem.at[f])
 
     def down_copy(j, f):
-        return pltpu.make_async_copy(w2.at[j, :, pl.ds(f * DCH, DCH)], b2.at[f], w2_sem.at[f])
+        return pltpu.make_async_copy(w2.at[j, :, pl.ds(pl.multiple_of(f * DCH, DCH), DCH)], b2.at[f], w2_sem.at[f])
 
     for f in range(NCH):
         up_copy(0, f).start()
@@ -403,9 +409,19 @@
         pl.semaphore_signal(barrier, inc=1, device_id={"ep": lax.rem(me + k, GROUP)}, device_id_type=MESH)
     pl.semaphore_wait(barrier, GROUP - 1)
 
+    if pooled:
+        over = pltpu.make_async_remote_copy(src_ref=ov_ref, dst_ref=pool.at[0], send_sem=e_send.at[0], recv_sem=e_recv.at[0],
+                                            device_id={"ep": me + 1 - 2 * lax.rem(me, 2)}, device_id_type=MESH)
+        over.start()
+        over.wait()
+        pool[1] = ye_ref[:, :EXTRA, :] + pool[0]
+        out_e = pool.at[1]
+    else:
+        out_e = ye_ref
+
     def e_copy(k):
         to = lax.rem(me + k, GROUP)
-        return pltpu.make_async_remote_copy(src_ref=ye_ref.at[to, pl.ds(0, cap), :], dst_ref=land_e.at[me], send_sem=e_send.at[k], recv_sem=e_recv.at[k],
+        return pltpu.make_async_remote_copy(src_ref=out_e.at[to, pl.ds(0, cap), :], dst_ref=land_e.at[me], send_sem=e_send.at[k], recv_sem=e_recv.at[k],
                                             device_id={"ep": to}, device_id_type=MESH)
 
     def b_copy(j, k):
@@ -417,14 +433,14 @@
 
     for k in range(1, GROUP):
         e_copy(k).start()
-    land_e[me] = ye_ref[me, :cap, :]
+    land_e[me] = out_e[me, :cap, :]
 
     def expert(j, carry):
-        x = xb_ref[j]
-        for f in range(NCH):
+        def up_step(f, c):
             up_copy(j, f).wait()
+            x = xb_ref[j]
             for p in range(FCH // 256):
-                cols = pl.ds(f * FCH + p * 256, 256)
+                cols = pl.ds(pl.multiple_of(f * FCH + p * 256, 256), 256)
                 up = dot(x, w1[j, :, cols])
                 lin = dot(x, b3[f, :, p * 256:(p + 1) * 256])
                 mid[:, cols] = (jax.nn.silu(up) * lin).astype(BF16)
@@ -432,13 +448,19 @@
             @pl.when(j + 1 < LOCAL)
             def _():
                 up_copy(j + 1, f).start()
-        for f in range(NCH):
+            return c
+
+        def down_step(f, c):
             down_copy(j, f).wait()
-            yb[j, :, f * DCH:(f + 1) * DCH] = dot(mid[...], b2[f]).astype(BF16)
+            yb[j, :, pl.ds(pl.multiple_of(f * DCH, DCH), DCH)] = dot(mid[...], b2[f]).astype(BF16)
 
             @pl.when(j + 1 < LOCAL)
             def _():
                 down_copy(j + 1, f).start()
+            return c
+
+        lax.fori_loop(0, NCH, up_step, 0)
+        lax.fori_loop(0, NCH, down_step, 0)
         land_b[me, pl.ds(pl.multiple_of(j * BASE, BASE), BASE), :] = yb[j, pl.ds(pl.multiple_of(me * BASE, BASE), BASE), :]
         for k in range(1, GROUP):
             b_copy(j, k).start()
@@ -446,41 +468,57 @@
 
     lax.fori_loop(0, LOCAL, expert, 0)
 
-    def table(field, start, size):
+    wr = wr_ref[...]
+    hb = h_ref[...]
+    w_hi = wr.astype(BF16)
+    rest = wr - w_hi.astype(F32)
+    w_mid = rest.astype(BF16)
+    w_lo = (rest - w_mid.astype(F32)).astype(BF16)
+    logits = dot_t(w_hi, hb) + (dot_t(w_mid, hb) + dot_t(w_lo, hb))
+    prob = jnp.exp(logits - jnp.max(logits, axis=0, keepdims=True))
+    prob = prob / jnp.sum(prob, axis=0, keepdims=True)
+    e_iota = lax.broadcasted_iota(I32, (EXPERTS, TOK), 0)
+    pick0 = jnp.sum(jnp.where(e_iota == ids_ref[0:1, :], prob, 0.0), axis=0, keepdims=True)
+    pick1 = jnp.sum(jnp.where(e_iota == ids_ref[1:2, :], prob, 0.0), axis=0, keepdims=True)
+    both = pick0 + pick1
+    gates = jnp.concatenate([pick0 / both, pick1 / both, jnp.zeros((126, TOK), F32)], axis=0).T
+
+    def table(own, field, start, size):
         place = tab_ref[:, field:field + 1]
         inside = (place >= start) & (place < start + size)
-        col = jnp.where(inside, tab_ref[:, field // 4 * 4:field // 4 * 4 + 1] * size + place - start, -1.0).astype(I32)
+        col = jnp.where(inside, tab_ref[:, own:own + 1] * size + place - start, -1.0).astype(I32)
         return (col == lax.broadcasted_iota(I32, (TOK, GROUP * size), 1)).astype(F32).astype(BF16)
 
     for k in range(1, GROUP):
         e_copy(k).wait()
     far = land_e[...].reshape(GROUP * cap, WIDTH)
-    mix0[...] = dot(table(2, 0, cap), far)
-    mix1[...] = dot(table(6, 0, cap), far)
+    own_at, pos_at = (3, 4) if pooled else (0, 2)
+    mix0[...] = dot(table(own_at, pos_at, 0, cap), far)
+    mix1[...] = dot(table(FIELDS + own_at, FIELDS + pos_at, 0, cap), far)
     early = (LOCAL - 1) * BASE
     for first, size in ((0, early), (early, BASE)):
         for j in range(first // BASE, (first + size) // BASE):
             for k in range(1, GROUP):
                 b_copy(j, k).wait()
         near = land_b[:, first:first + size, :].reshape(GROUP * size, WIDTH)
-        y0 = mix0[...] + dot(table(1, first, size), near)
-        y1 = mix1[...] + dot(table(5, first, size), near)
+        y0 = mix0[...] + dot(table(0, 1, first, size), near)
+        y1 = mix1[...] + dot(table(FIELDS, FIELDS + 1, first, size), near)
         if first == 0:
             mix0[...] = y0
             mix1[...] = y1
-    mixed = tab_ref[:, 3:4] * y0 + tab_ref[:, 7:8] * y1
+    mixed = gates[:, 0:1] * y0 + gates[:, 1:2] * y1
     out_ref[...] = (scale[0] * h_ref[...].astype(F32) + scale[1] * mixed).astype(BF16)
 
 
-def base(index, cap, scale, tab, hidden, xb, ye, w1, w3, w2):
+def base(index, cap, pooled, scale, ids_t, wr_t, tab, hidden, xb, ye, ov, w1, w3, w2):
     vmem = pl.BlockSpec(memory_space=pltpu.VMEM)
     hbm = pl.BlockSpec(memory_space=pl.ANY)
     dma = pltpu.SemaphoreType.DMA
     return pl.pallas_call(
-        functools.partial(base_kernel, cap),
-        name=f"base_rows_{cap}",
+        functools.partial(base_kernel, cap, pooled),
+        name=f"base_{cap}{'_pooled' if pooled else ''}",
         out_shape=jax.ShapeDtypeStruct((TOK, WIDTH), BF16),
-        in_specs=[pl.BlockSpec(memory_space=pltpu.SMEM)] + [vmem] * 5 + [hbm] * 2,
+        in_specs=[pl.BlockSpec(memory_space=pltpu.SMEM)] + [vmem] * 8 + [hbm] * 2,
         out_specs=vmem,
         scratch_shapes=[
             pltpu.VMEM((GROUP, cap, WIDTH), BF16),
@@ -491,19 +529,22 @@
             pltpu.VMEM((RING, FFN, DCH), BF16),
             pltpu.VMEM((TOK, WIDTH), F32),
             pltpu.VMEM((TOK, WIDTH), F32),
+            pltpu.VMEM((2, GROUP, EXTRA if pooled else 16, WIDTH), BF16),
             dma((RING,)), dma((RING,)),
             dma((GROUP,)), dma((GROUP,)), dma((LOCAL, GROUP)), dma((LOCAL, GROUP)),
         ],
         compiler_params=pltpu.CompilerParams(collective_id=2 + index, has_side_effects=True, vmem_limit_bytes=BASE_VMEM * 2**20),
-    )(scale, tab, hidden, xb, ye, w1, w3, w2)
+    )(scale, ids_t, wr_t, tab, hidden, xb, ye, ov, w1, w3, w2)
 
 
 def solution(mesh):
     def local_step(hidden, router_w, expert_ids, w_gate, w_up, w_down, post_scale):
-        xb, xe, cnt, tab, top = gather(expert_ids.T, hidden, router_w.T)
-        ye = extra(cnt, xe, w_gate, w_up, w_down)
-        branches = [functools.partial(base, i, cap) for i, cap in enumerate(BUCKETS)]
-        return lax.switch(top[0, 0], branches, post_scale, tab, hidden, xb, ye, w_gate, w_up, w_down)
+        ids_t, wr_t = expert_ids.T, router_w.T
+        xb, xe, cnt, tab, top = gather(ids_t, hidden)
+        ye, ov = extra(cnt, xe, w_gate, w_up, w_down)
+        plans = [(EXTRA, False), (EXTRA, True)] + [(cap, False) for cap in BUCKETS[1:]]
+        branches = [functools.partial(base, i, cap, pooled) for i, (cap, pooled) in enumerate(plans)]
+        return lax.switch(top[0, 0], branches, post_scale, ids_t, wr_t, tab, hidden, xb, ye, ov, w_gate, w_up, w_down)
 
     tok_spec = P(("dp", "ep"))
     return jax.shard_map(local_step, mesh=mesh, in_specs=(tok_spec, P(), tok_spec, P("ep"), P("ep"), P("ep"), P()), out_specs=tok_spec, check_vma=False)

time: 86 us -> 84.9 us (0.987)
  local copies, waits for them, and re-layouts: 3.02 us -> 1.45 us
    unnamed x11 -> x23, local copies, waits for them, and re-layouts: 2.51 us -> 0.94 us
where the time goes in v1:
time: 84.9 us; the launch traced here: 84.8 us
  Pallas kernels  81.8 us (96%)
  local copies, waits for them, and re-layouts  1.45 us (2%)
    pallas_call x1, Pallas kernels, base(): pl.pallas_call(functools.partial(base_kernel, cap, pooled), name=f"base_{...  45.8 us
    pallas_call x1, Pallas kernels, gather(): pl.pallas_call(gather_kernel, name='gather_rows', out_shape=[jax.ShapeDty...  33.3 us
    pallas_call x1, Pallas kernels, extra(): pl.pallas_call(extra_kernel, name='extra_rows', out_shape=[jax.ShapeDtype...  2.68 us

profile of v1, /device:TPU:0, one launch (start us, length us, event | category | flops | bytes accessed | tf_op | source)
XLA Modules:
  0.0 84.8 jit_solution(16483686542377590780)
XLA Ops:
  0.0 0.0 slice-start
  0.0 0.0 slice-start.1
  0.0 0.0 slice-start.2
  0.0 0.0 slice-start.3
  0.0 0.0 slice-start.4
  0.0 0.0 slice-start.5
  0.0 0.0 slice-start.6
  0.0 33.3 %gather_rows.1 = (bf16[4,128,1536]{2,1,0:T(8,128)(2,1)S(1)}, bf16[8,192,1536]{2,1,0:T(8,128)(2,1)S(1)}, s32[8,64]{1,0:T(8,128)S(1)}, f32[256,128]{1,0:T(8,128)S(1)}, s32[8,128]{1,0:T(8,128)S(1)}) custom-call(s32[2,256]{1,0:T(2,128)} %bitcast.10, bf16[256,1536]{1,0:T(8,128)(2,1)} %h_hbm.1), custom_call_target="tpu_custom_call" | custom-call | flops 20000000000 | bytes 20000000 | tf_op jit(solution)/shard_map/gather_rows/pallas_call | solution.py:218
  33.3 0.5 slice.3
  34.5 0.0 slice-done
  34.5 0.0 slice-done.1
  34.5 0.0 slice-done.2
  34.5 0.0 slice-done.3
  34.5 0.0 slice-done.4
  34.5 0.0 slice-done.5
  34.5 0.0 slice-done.6
  34.5 0.0 copy-start
  34.6 0.0 copy-start.1
  34.6 0.0 copy-start.2
  34.6 0.0 copy-start.3
  34.6 2.7 %extra_rows.1 = (bf16[8,192,1536]{2,1,0:T(8,128)(2,1)S(1)}, bf16[8,48,1536]{2,1,0:T(8,128)(2,1)S(1)}) custom-call(s32[8,64]{1,0:T(8,128)S(1)} %get-tuple-element.186.cnt, bf16[8,192,1536]{2,1,0:T(8,128)(2,1)S(1)} %get-tuple-element.187.xe_ref, bf16[4,1536,2304]{2,1,0:T(8,128)(2,1)S(1)} %bitcast.4, ...), custom_call_target="tpu_custom_call", output_to_operand_aliasing={{0}: (1, {})} | custom-call | flops 8000000000 | bytes 30000000 | tf_op jit(solution)/shard_map/extra_rows/pallas_call | solution.py:370
  37.3 0.0 copy-done
  37.3 0.0 copy-done.1
  37.3 0.0 copy-done.2
  37.3 0.0 copy-done.3
  37.3 46.6 %conditional.1 = (bf16[256,1536]{1,0:T(8,128)(2,1)S(1)}) conditional(s32[]{:T(128)} %bitcast.1, (f32[2]{0:T(128)S(1)}, s32[2,256]{1,0:T(2,128)S(1)}, f32[32,1536]{1,0:T(8,128)S(1)}, f32[256,128]{1,0:T(8,128)S(1)}, bf16[256,1536]{1,0:T(8,128)(2,1)S(1)}, /*index=5*/bf16[4,128,1536]{2,1,0:T(8,128)(2,1)S(1)}, ...), branch_computations={%region_0.0_spmd, %region_1.0_spmd, %region_2.0_spmd, %region_3.0_... | conditional | bytes 8 | solution.py:547
  37.5 45.8 %base_48.1 = bf16[256,1536]{1,0:T(8,128)(2,1)S(1)} custom-call(f32[2]{0:T(128)S(1)} %get-tuple-element.98.scale, s32[2,256]{1,0:T(2,128)S(1)} %get-tuple-element.120.ids_ref, f32[32,1536]{1,0:T(8,128)S(1)} %get-tuple-element.122.wr_ref, f32[256,128]{1,0:T(8,128)S(1)} %get-tuple-element.124.tab_ref, bf16[256,1536]{1,0:T(8,128)(2,1)S(1)} %get-tuple-element.125.h_ref, ...), custom_call_target="tpu_custom_call" | custom-call | tf_op jit(solution)/shard_map/cond/branch_0_fun/base_48/pallas_call | solution.py:517
  83.9 0.9 %copy.21 = bf16[256,1536]{1,0:T(8,128)(2,1)} copy(bf16[256,1536]{1,0:T(8,128)(2,1)S(1)} %get-tuple-element.190) | data formatting | bytes 1572864
  (1 shorter events, 0.0 us)
Async XLA Ops:
  0.0 34.5 %slice-start = ((s8[28311552]{0:T(1024)(128)(4,1)}), s8[4194304]{0:T(1024)(128)(4,1)S(1)}, s32[]{:S(2)}) async-start(s8[28311552]{0:T(1024)(128)(4,1)} %bitcast.3), calls=%async_computation | async-start | bytes 8388608
  0.0 34.5 %slice-start.1 = ((s8[28311552]{0:T(1024)(128)(4,1)}), s8[4194304]{0:T(1024)(128)(4,1)S(1)}, s32[]{:S(2)}) async-start(s8[28311552]{0:T(1024)(128)(4,1)} %bitcast.3), calls=%async_computation.1 | async-start | bytes 8388608
  0.0 34.5 %slice-start.2 = ((s8[28311552]{0:T(1024)(128)(4,1)}), s8[4194304]{0:T(1024)(128)(4,1)S(1)}, s32[]{:S(2)}) async-start(s8[28311552]{0:T(1024)(128)(4,1)} %bitcast.3), calls=%async_computation.2 | async-start | bytes 8388608
  0.0 34.5 %slice-start.3 = ((s8[28311552]{0:T(1024)(128)(4,1)}), s8[4194304]{0:T(1024)(128)(4,1)S(1)}, s32[]{:S(2)}) async-start(s8[28311552]{0:T(1024)(128)(4,1)} %bitcast.3), calls=%async_computation.3 | async-start | bytes 8388608
  0.0 34.5 %slice-start.4 = ((s8[28311552]{0:T(1024)(128)(4,1)}), s8[4194304]{0:T(1024)(128)(4,1)S(1)}, s32[]{:S(2)}) async-start(s8[28311552]{0:T(1024)(128)(4,1)} %bitcast.3), calls=%async_computation.4 | async-start | bytes 8388608
  0.0 34.5 %slice-start.5 = ((s8[28311552]{0:T(1024)(128)(4,1)}), s8[4194304]{0:T(1024)(128)(4,1)S(1)}, s32[]{:S(2)}) async-start(s8[28311552]{0:T(1024)(128)(4,1)} %bitcast.3), calls=%async_computation.5 | async-start | bytes 8388608
  0.0 34.5 %slice-start.6 = ((s8[28311552]{0:T(1024)(128)(4,1)}), s8[3145728]{0:T(1024)(128)(4,1)S(1)}, s32[]{:S(2)}) async-start(s8[28311552]{0:T(1024)(128)(4,1)} %bitcast.3), calls=%async_computation.6 | async-start | bytes 6291456
  34.5 2.7 %copy-start = (bf16[256,1536]{1,0:T(8,128)(2,1)S(1)}, bf16[256,1536]{1,0:T(8,128)(2,1)}, u32[]{:S(2)}) copy-start(bf16[256,1536]{1,0:T(8,128)(2,1)} %h_hbm.1) | copy-start | bytes 2359300
  34.6 2.7 %copy-start.1 = (f32[1536,32]{0,1:T(8,128)S(1)}, f32[1536,32]{0,1:T(8,128)}, u32[]{:S(2)}) copy-start(f32[1536,32]{0,1:T(8,128)} %param.13) | copy-start | bytes 589828
  34.6 2.7 %copy-start.2 = (s32[256,2]{0,1:T(2,128)S(1)}, s32[256,2]{0,1:T(2,128)}, u32[]{:S(2)}) copy-start(s32[256,2]{0,1:T(2,128)} %param.14) | copy-start | bytes 6148
  34.6 2.7 %copy-start.3 = (f32[2]{0:T(128)S(1)}, f32[2]{0:T(128)}, u32[]{:S(2)}) copy-start(f32[2]{0:T(128)} %param.18) | copy-start | bytes 28

commit v2 on v1

--- a/solution.py
+++ b/solution.py
@@ -28,7 +28,7 @@
 XROWS = GROUP * EXTRA + 128
 FIELDS = 5
 GATHER_VMEM = 15
-EXPERT_VMEM = 24
+EXPERT_VMEM = 20
 BASE_VMEM = 27
 
 
@@ -45,7 +45,7 @@
     return jnp.floor((over + 15.0) * (1.0 / 16.0)) * 16.0
 
 
-def gather_kernel(ids_hbm, h_hbm, xb_ref, xe_ref, cnt_ref, tab_ref, top_ref,
+def gather_kernel(ids_hbm, h_hbm, xb_ref, xe_ref, cnt_ref, tab_ref,
                   ids_ref, h_ref, in_sem, hall, rk, idbuf, needs, id_send, id_recv, x_send, y_send, p_send, x_recv, y_recv, d_recv, p_recv, own_sem):
     dp, me = lax.axis_index("dp"), lax.axis_index("ep")
     core, xc, yc = lax.rem(me, 2), lax.rem(me // 2, 2), me // 4
@@ -136,7 +136,7 @@
     hit_f = jnp.where(jnp.concatenate(hit_list, axis=0), 1.0, 0.0)
     hit_b = hit_f.astype(BF16)
     rk[...] = jnp.where(hit_f > 0.5, dot(hit_b, upper), -1.0).astype(I32).reshape(GROUP, 8, TOK)
-    cnt_ref[...] = dot_t(jnp.ones((8, TOK), BF16), hit_b).astype(I32)
+    cnt_ref[:, 0:GROUP * 8] = extra_rows(dot_t(jnp.ones((8, TOK), BF16), hit_b)).astype(I32)
     lane = lax.broadcasted_iota(I32, (EXPERTS, 128), 1)
     spread = jnp.zeros((EXPERTS, 128), F32)
     for g in range(GROUP):
@@ -207,7 +207,8 @@
     other.wait()
     need, pooled = jnp.maximum(needs[0, 0], needs[1, 0]), jnp.maximum(needs[0, 1], needs[1, 1])
     rest = sum((need > cap).astype(I32) for cap in BUCKETS[1:-1]) + 2
-    top_ref[...] = jnp.where(need <= EXTRA, 0, jnp.where((pooled <= EXTRA) & (need <= 2 * EXTRA), 1, rest))
+    index = jnp.where(need <= EXTRA, 0, jnp.where((pooled <= EXTRA) & (need <= 2 * EXTRA), 1, rest))
+    cnt_ref[:, GROUP * 8:] = index[:, GROUP * 8:]
     for copy in sends:
         copy.wait_send()
 
@@ -221,12 +222,11 @@
         out_shape=[
             jax.ShapeDtypeStruct((LOCAL, BROWS, WIDTH), BF16),
             jax.ShapeDtypeStruct((GROUP, LOCAL * EXTRA, WIDTH), BF16),
-            jax.ShapeDtypeStruct((8, GROUP * 8), I32),
+            jax.ShapeDtypeStruct((8, 128), I32),
             jax.ShapeDtypeStruct((TOK, 128), F32),
-            jax.ShapeDtypeStruct((8, 128), I32),
         ],
         in_specs=[pl.BlockSpec(memory_space=pltpu.HBM)] * 2,
-        out_specs=[vmem] * 5,
+        out_specs=[vmem] * 4,
         scratch_shapes=[
             pltpu.VMEM((2, TOK), I32),
             pltpu.VMEM((TOK, WIDTH), BF16),
@@ -245,20 +245,17 @@
     )(ids_t, hidden)
 
 
-def extra_kernel(cnt, xe_ref, w1, w3, w2, ye_ref, ov_ref, xbuf, mid, b3, b2, offs, act, tot, w3_sem, w2_sem):
+def extra_kernel(cnt, xe_ref, w1, w3, w2, ye_ref, ov_ref, top_ref, xbuf, mid, b3, b2, act, pos, w3_sem, w2_sem):
     def tiles(s, j):
-        return (jnp.maximum(cnt[0, s * 8 + j] - BASE, 0) + 15) // 16 * 16
+        return cnt[0, s * 8 + j]
 
     active = jnp.int32(0)
     for j in range(LOCAL):
-        at = jnp.int32(0)
-        for s in range(GROUP):
-            offs[s, j] = at
-            at = at + tiles(s, j)
-        tot[j] = at
         act[active] = j
-        active = active + (at > 0).astype(I32)
+        active = active + jnp.minimum(sum(tiles(s, j) for s in range(GROUP)), 1)
     chunks = active * NCH
+    index = cnt[0, GROUP * 8]
+    top_ref[0] = index
 
     def up_copy(g):
         slot = lax.rem(g, RING)
@@ -280,22 +277,26 @@
     for g in range(RING):
         fetch(down_copy, g)
 
-    def compact(s, carry):
-        for j in range(LOCAL):
-            @pl.when(tot[j] > 0)
-            def _():
-                xbuf[j, pl.ds(pl.multiple_of(offs[s, j], 16), EXTRA), :] = xe_ref[s, j * EXTRA:(j + 1) * EXTRA, :]
-        return carry
-
-    lax.fori_loop(0, GROUP, compact, 0)
-    ye_ref[...] = jnp.zeros_like(ye_ref)
-    ov_ref[...] = jnp.zeros_like(ov_ref)
+    ye_ref[:, :EXTRA, :] = jnp.zeros((GROUP, EXTRA, WIDTH), BF16)
+    for s in range(GROUP):
+        pos[s] = 0
+
+    @pl.when(index == 1)
+    def _():
+        ov_ref[...] = jnp.zeros_like(ov_ref)
+
+    @pl.when(index > 1)
+    def _():
+        ye_ref[:, EXTRA:, :] = jnp.zeros((GROUP, (LOCAL - 1) * EXTRA, WIDTH), BF16)
 
     def expert(a, carry):
         j = act[a]
-        total = tot[j]
+        total = jnp.int32(0)
+        for s in range(GROUP):
+            xbuf[pl.ds(pl.multiple_of(total, 16), EXTRA), :] = xe_ref[s, pl.ds(pl.multiple_of(j * EXTRA, 16), EXTRA), :]
+            total = total + tiles(s, j)
         blocks = (total + 127) // 128
-        xbuf[j, pl.ds(pl.multiple_of(total, 16), 128), :] = jnp.zeros((128, WIDTH), BF16)
+        xbuf[pl.ds(pl.multiple_of(total, 16), 128), :] = jnp.zeros((128, WIDTH), BF16)
 
         def over_rows(body):
             for n in range(1, 4):
@@ -309,7 +310,7 @@
             up_copy(g).wait()
 
             def body(n):
-                x = xbuf[j, :n, :]
+                x = xbuf[:n, :]
                 for p in range(FCH // 256):
                     cols = pl.ds(pl.multiple_of(f * FCH + p * 256, 256), 256)
                     up = dot(x, w1[j, :, cols])
@@ -327,7 +328,7 @@
 
             def body(n):
                 cols = pl.ds(pl.multiple_of(f * DCH, DCH), DCH)
-                xbuf[j, :n, cols] = dot(mid[:n, :], b2[slot]).astype(BF16)
+                xbuf[:n, cols] = dot(mid[:n, :], b2[slot]).astype(BF16)
 
             over_rows(body)
             fetch(down_copy, g + RING)
@@ -335,32 +336,33 @@
 
         lax.fori_loop(0, NCH, up_step, 0)
         lax.fori_loop(0, NCH, down_step, 0)
+        at = jnp.int32(0)
+        for s in range(GROUP):
+            put = pos[s]
+            ye_ref[s, pl.ds(pl.multiple_of(put, 16), EXTRA), :] = xbuf[pl.ds(pl.multiple_of(at, 16), EXTRA), :]
+            at = at + tiles(s, j)
+            pos[s] = put + tiles(s, j)
         return carry
 
     lax.fori_loop(0, active, expert, 0)
 
-    def pack(s, carry):
-        at = jnp.int32(0)
-        for j in range(LOCAL):
-            n = tiles(s, j)
-
-            @pl.when(n > 0)
+    @pl.when(index == 1)
+    def _():
+        def pool(s, carry):
+            own = pos[s]
+
+            @pl.when(own < EXTRA)
             def _():
-                ye_ref[s, pl.ds(pl.multiple_of(at, 16), EXTRA), :] = xbuf[j, pl.ds(pl.multiple_of(offs[s, j], 16), EXTRA), :]
-            at = at + n
-
-        @pl.when(at <= (LOCAL - 1) * EXTRA)
-        def _():
-            ye_ref[s, pl.ds(pl.multiple_of(at, 16), EXTRA), :] = jnp.zeros((EXTRA, WIDTH), BF16)
-
-        behind = jnp.minimum(sum(tiles(s, LOCAL + j) for j in range(LOCAL)), EXTRA)
-        for t in range(EXTRA // 16):
-            @pl.when((at > EXTRA + 16 * t) & (behind + 16 * t < EXTRA))
-            def _():
-                ov_ref[s, pl.ds(pl.multiple_of(behind + 16 * t, 16), 16), :] = ye_ref[s, EXTRA + 16 * t:EXTRA + 16 * (t + 1), :]
-        return carry
-
-    lax.fori_loop(0, GROUP, pack, 0)
+                ye_ref[s, pl.ds(pl.multiple_of(own, 16), EXTRA), :] = jnp.zeros((EXTRA, WIDTH), BF16)
+
+            behind = jnp.minimum(sum(tiles(s, LOCAL + j) for j in range(LOCAL)), EXTRA)
+            for t in range(EXTRA // 16):
+                @pl.when((own > EXTRA + 16 * t) & (behind + 16 * t < EXTRA))
+                def _():
+                    ov_ref[s, pl.ds(pl.multiple_of(behind + 16 * t, 16), 16), :] = ye_ref[s, EXTRA + 16 * t:EXTRA + 16 * (t + 1), :]
+            return carry
+
+        lax.fori_loop(0, GROUP, pool, 0)
 
 
 def extra(cnt, xe, w1, w3, w2):
@@ -370,18 +372,17 @@
     return pl.pallas_call(
         extra_kernel,
         name="extra_rows",
-        out_shape=[jax.ShapeDtypeStruct((GROUP, LOCAL * EXTRA, WIDTH), BF16), jax.ShapeDtypeStruct((GROUP, EXTRA, WIDTH), BF16)],
+        out_shape=[jax.ShapeDtypeStruct((GROUP, LOCAL * EXTRA, WIDTH), BF16), jax.ShapeDtypeStruct((GROUP, EXTRA, WIDTH), BF16),
+                   jax.ShapeDtypeStruct((1,), I32)],
         in_specs=[pl.BlockSpec(memory_space=pltpu.SMEM), vmem, vmem, hbm, hbm],
-        out_specs=[vmem] * 2,
-        input_output_aliases={1: 0},
+        out_specs=[vmem] * 2 + [pl.BlockSpec(memory_space=pltpu.SMEM)],
         scratch_shapes=[
-            pltpu.VMEM((LOCAL, XROWS, WIDTH), BF16),
+            pltpu.VMEM((XROWS, WIDTH), BF16),
             pltpu.VMEM((GROUP * EXTRA, FFN), BF16),
             pltpu.VMEM((RING, WIDTH, FCH), BF16),
             pltpu.VMEM((RING, FFN, DCH), BF16),
-            pltpu.SMEM((GROUP, LOCAL), I32),
             pltpu.SMEM((LOCAL + 1,), I32),
-            pltpu.SMEM((LOCAL,), I32),
+            pltpu.SMEM((GROUP,), I32),
             dma((RING,)), dma((RING,)),
         ],
         compiler_params=pltpu.CompilerParams(vmem_limit_bytes=EXPERT_VMEM * 2**20),
@@ -390,7 +391,7 @@
 
 
 def base_kernel(cap, pooled, scale, ids_ref, wr_ref, tab_ref, h_ref, xb_ref, ye_ref, ov_ref, w1, w3, w2, out_ref,
-                land_e, land_b, yb, mid, b3, b2, mix0, mix1, pool, w3_sem, w2_sem, e_send, e_recv, b_send, b_recv):
+                land_e, land_b, yb, mid, b3, b2, mix, pool, w3_sem, w2_sem, e_send, e_recv, b_send, b_recv):
     me = lax.axis_index("ep")
 
     def up_copy(j, f):
@@ -489,25 +490,25 @@
         col = jnp.where(inside, tab_ref[:, own:own + 1] * size + place - start, -1.0).astype(I32)
         return (col == lax.broadcasted_iota(I32, (TOK, GROUP * size), 1)).astype(F32).astype(BF16)
 
+    own_at, pos_at = (3, 4) if pooled else (0, 2)
+    early = (LOCAL - 1) * BASE
+    gate0, gate1 = scale[1] * gates[:, 0:1], scale[1] * gates[:, 1:2]
+    far0, far1 = table(own_at, pos_at, 0, cap), table(FIELDS + own_at, FIELDS + pos_at, 0, cap)
+    near0, near1 = table(0, 1, 0, early), table(FIELDS, FIELDS + 1, 0, early)
+    last0, last1 = table(0, 1, early, BASE), table(FIELDS, FIELDS + 1, early, BASE)
     for k in range(1, GROUP):
         e_copy(k).wait()
     far = land_e[...].reshape(GROUP * cap, WIDTH)
-    own_at, pos_at = (3, 4) if pooled else (0, 2)
-    mix0[...] = dot(table(own_at, pos_at, 0, cap), far)
-    mix1[...] = dot(table(FIELDS + own_at, FIELDS + pos_at, 0, cap), far)
-    early = (LOCAL - 1) * BASE
-    for first, size in ((0, early), (early, BASE)):
-        for j in range(first // BASE, (first + size) // BASE):
-            for k in range(1, GROUP):
-                b_copy(j, k).wait()
-        near = land_b[:, first:first + size, :].reshape(GROUP * size, WIDTH)
-        y0 = mix0[...] + dot(table(0, 1, first, size), near)
-        y1 = mix1[...] + dot(table(FIELDS, FIELDS + 1, first, size), near)
-        if first == 0:
-            mix0[...] = y0
-            mix1[...] = y1
-    mixed = gates[:, 0:1] * y0 + gates[:, 1:2] * y1
-    out_ref[...] = (scale[0] * h_ref[...].astype(F32) + scale[1] * mixed).astype(BF16)
+    mix[...] = scale[0] * h_ref[...].astype(F32) + (gate0 * dot(far0, far) + gate1 * dot(far1, far))
+    for j in range(LOCAL - 1):
+        for k in range(1, GROUP):
+            b_copy(j, k).wait()
+    near = land_b[:, :early, :].reshape(GROUP * early, WIDTH)
+    mix[...] += gate0 * dot(near0, near) + gate1 * dot(near1, near)
+    for k in range(1, GROUP):
+        b_copy(LOCAL - 1, k).wait()
+    last = land_b[:, early:, :].reshape(GROUP * BASE, WIDTH)
+    out_ref[...] = (mix[...] + (gate0 * dot(last0, last) + gate1 * dot(last1, last))).astype(BF16)
 
 
 def base(index, cap, pooled, scale, ids_t, wr_t, tab, hidden, xb, ye, ov, w1, w3, w2):
@@ -528,7 +529,6 @@
             pltpu.VMEM((RING, WIDTH, FCH), BF16),
             pltpu.VMEM((RING, FFN, DCH), BF16),
             pltpu.VMEM((TOK, WIDTH), F32),
-            pltpu.VMEM((TOK, WIDTH), F32),
             pltpu.VMEM((2, GROUP, EXTRA if pooled else 16, WIDTH), BF16),
             dma((RING,)), dma((RING,)),
             dma((GROUP,)), dma((GROUP,)), dma((LOCAL, GROUP)), dma((LOCAL, GROUP)),
@@ -540,11 +540,11 @@
 def solution(mesh):
     def local_step(hidden, router_w, expert_ids, w_gate, w_up, w_down, post_scale):
         ids_t, wr_t = expert_ids.T, router_w.T
-        xb, xe, cnt, tab, top = gather(ids_t, hidden)
-        ye, ov = extra(cnt, xe, w_gate, w_up, w_down)
+        xb, xe, cnt, tab = gather(ids_t, hidden)
+        ye, ov, top = extra(cnt, xe, w_gate, w_up, w_down)
         plans = [(EXTRA, False), (EXTRA, True)] + [(cap, False) for cap in BUCKETS[1:]]
         branches = [functools.partial(base, i, cap, pooled) for i, (cap, pooled) in enumerate(plans)]
-        return lax.switch(top[0, 0], branches, post_scale, ids_t, wr_t, tab, hidden, xb, ye, ov, w_gate, w_up, w_down)
+        return lax.switch(top[0], branches, post_scale, ids_t, wr_t, tab, hidden, xb, ye, ov, w_gate, w_up, w_down)
 
     tok_spec = P(("dp", "ep"))
     return jax.shard_map(local_step, mesh=mesh, in_specs=(tok_spec, P(), tok_spec, P("ep"), P("ep"), P("ep"), P()), out_specs=tok_spec, check_vma=False)

time: 84.9 us -> 83.4 us (0.982)
  Pallas kernels: 81.8 us -> 80.6 us
    pallas_call x1, Pallas kernels: 45.8 us -> 34.9 us  [base(): pl.pallas_call(functools.partial(base_kernel, cap, pooled), name=f"base_{...]
    pallas_call x1, Pallas kernels: 2.68 us -> 12.5 us  [extra(): pl.pallas_call(extra_kernel, name='extra_rows', out_shape=[jax.ShapeDtype...]
where the time goes in v2:
time: 83.4 us; the launch traced here: 83.1 us
  Pallas kernels  80.6 us (97%)
  local copies, waits for them, and re-layouts  0.94 us (1%)
    pallas_call x1, Pallas kernels, base(): pl.pallas_call(functools.partial(base_kernel, cap, pooled), name=f"base_{...  34.9 us
    pallas_call x1, Pallas kernels, gather(): pl.pallas_call(gather_kernel, name='gather_rows', out_shape=[jax.ShapeDty...  33.3 us
    pallas_call x1, Pallas kernels, extra(): pl.pallas_call(extra_kernel, name='extra_rows', out_shape=[jax.ShapeDtype...  12.5 us

profile of v2, /device:TPU:0, one launch (start us, length us, event | category | flops | bytes accessed | tf_op | source)
XLA Modules:
  0.0 83.1 jit_solution(9474842256530762589)
XLA Ops:
  0.0 0.0 slice-start
  0.0 0.0 slice-start.1
  0.0 0.0 slice-start.2
  0.0 0.0 slice-start.3
  0.0 0.0 slice-start.4
  0.0 0.0 slice-start.5
  0.0 0.0 slice-start.6
  0.0 33.3 %gather_rows.1 = (bf16[4,128,1536]{2,1,0:T(8,128)(2,1)S(1)}, bf16[8,192,1536]{2,1,0:T(8,128)(2,1)S(1)}, s32[8,128]{1,0:T(8,128)S(1)}, f32[256,128]{1,0:T(8,128)S(1)}) custom-call(s32[2,256]{1,0:T(2,128)} %bitcast.10, bf16[256,1536]{1,0:T(8,128)(2,1)} %h_hbm.1), custom_call_target="tpu_custom_call" | custom-call | flops 20000000000 | bytes 20000000 | tf_op jit(solution)/shard_map/gather_rows/pallas_call | solution.py:219
  33.3 0.0 slice-done
  33.3 0.0 slice-done.1
  33.3 0.0 slice-done.2
  33.3 0.0 slice-done.3
  33.3 0.0 slice-done.4
  33.3 0.0 slice-done.5
  33.4 0.0 slice-done.6
  33.4 0.0 copy-start
  33.4 0.0 copy-start.1
  33.4 0.0 copy-start.2
  33.4 0.0 copy-start.3
  33.4 12.5 %extra_rows.1 = (bf16[8,192,1536]{2,1,0:T(8,128)(2,1)S(1)}, bf16[8,48,1536]{2,1,0:T(8,128)(2,1)S(1)}, s32[1]{0:T(128)}) custom-call(s32[8,128]{1,0:T(8,128)S(1)} %get-tuple-element.183.cnt, bf16[8,192,1536]{2,1,0:T(8,128)(2,1)S(1)} %get-tuple-element.184.xe_ref, bf16[4,1536,2304]{2,1,0:T(8,128)(2,1)S(1)} %bitcast.4, bf16[4,1536,2304]{2,1,0:T(8,128)(2,1)} %w3.1, ...), custom_call_target="tpu_custom_call" | custom-call | flops 8000000000 | bytes 30000000 | tf_op jit(solution)/shard_map/extra_rows/pallas_call | solution.py:372
  46.5 0.0 copy-done
  46.6 0.0 copy-done.1
  46.6 0.0 copy-done.2
  46.6 0.0 copy-done.3
  46.6 35.6 %conditional.1 = (bf16[256,1536]{1,0:T(8,128)(2,1)S(1)}) conditional(s32[]{:T(128)} %bitcast.1, (f32[2]{0:T(128)S(1)}, s32[2,256]{1,0:T(2,128)S(1)}, f32[32,1536]{1,0:T(8,128)S(1)}, f32[256,128]{1,0:T(8,128)S(1)}, bf16[256,1536]{1,0:T(8,128)(2,1)S(1)}, /*index=5*/bf16[4,128,1536]{2,1,0:T(8,128)(2,1)S(1)}, ...), branch_computations={%region_0.0_spmd, %region_1.0_spmd, %region_2.0_spmd, %region_3.0_... | conditional | bytes 8 | solution.py:547
  46.8 34.9 %base_48.1 = bf16[256,1536]{1,0:T(8,128)(2,1)S(1)} custom-call(f32[2]{0:T(128)S(1)} %get-tuple-element.98.scale, s32[2,256]{1,0:T(2,128)S(1)} %get-tuple-element.120.ids_ref, f32[32,1536]{1,0:T(8,128)S(1)} %get-tuple-element.122.wr_ref, f32[256,128]{1,0:T(8,128)S(1)} %get-tuple-element.124.tab_ref, bf16[256,1536]{1,0:T(8,128)(2,1)S(1)} %get-tuple-element.125.h_ref, ...), custom_call_target="tpu_custom_call" | custom-call | tf_op jit(solution)/shard_map/cond/branch_0_fun/base_48/pallas_call | solution.py:518
  82.2 0.9 %copy.19 = bf16[256,1536]{1,0:T(8,128)(2,1)} copy(bf16[256,1536]{1,0:T(8,128)(2,1)S(1)} %get-tuple-element.190) | data formatting | bytes 1572864
  (1 shorter events, 0.0 us)
Async XLA Ops:
  0.0 33.3 %slice-start = ((s8[28311552]{0:T(1024)(128)(4,1)}), s8[4194304]{0:T(1024)(128)(4,1)S(1)}, s32[]{:S(2)}) async-start(s8[28311552]{0:T(1024)(128)(4,1)} %bitcast.3), calls=%async_computation | async-start | bytes 8388608
  0.0 33.3 %slice-start.1 = ((s8[28311552]{0:T(1024)(128)(4,1)}), s8[4194304]{0:T(1024)(128)(4,1)S(1)}, s32[]{:S(2)}) async-start(s8[28311552]{0:T(1024)(128)(4,1)} %bitcast.3), calls=%async_computation.1 | async-start | bytes 8388608
  0.0 33.3 %slice-start.2 = ((s8[28311552]{0:T(1024)(128)(4,1)}), s8[4194304]{0:T(1024)(128)(4,1)S(1)}, s32[]{:S(2)}) async-start(s8[28311552]{0:T(1024)(128)(4,1)} %bitcast.3), calls=%async_computation.2 | async-start | bytes 8388608
  0.0 33.3 %slice-start.3 = ((s8[28311552]{0:T(1024)(128)(4,1)}), s8[4194304]{0:T(1024)(128)(4,1)S(1)}, s32[]{:S(2)}) async-start(s8[28311552]{0:T(1024)(128)(4,1)} %bitcast.3), calls=%async_computation.3 | async-start | bytes 8388608
  0.0 33.3 %slice-start.4 = ((s8[28311552]{0:T(1024)(128)(4,1)}), s8[4194304]{0:T(1024)(128)(4,1)S(1)}, s32[]{:S(2)}) async-start(s8[28311552]{0:T(1024)(128)(4,1)} %bitcast.3), calls=%async_computation.4 | async-start | bytes 8388608
  0.0 33.3 %slice-start.5 = ((s8[28311552]{0:T(1024)(128)(4,1)}), s8[4194304]{0:T(1024)(128)(4,1)S(1)}, s32[]{:S(2)}) async-start(s8[28311552]{0:T(1024)(128)(4,1)} %bitcast.3), calls=%async_computation.5 | async-start | bytes 8388608
  0.0 33.3 %slice-start.6 = ((s8[28311552]{0:T(1024)(128)(4,1)}), s8[3145728]{0:T(1024)(128)(4,1)S(1)}, s32[]{:S(2)}) async-start(s8[28311552]{0:T(1024)(128)(4,1)} %bitcast.3), calls=%async_computation.6 | async-start | bytes 6291456
  33.4 13.2 %copy-start = (bf16[256,1536]{1,0:T(8,128)(2,1)S(1)}, bf16[256,1536]{1,0:T(8,128)(2,1)}, u32[]{:S(2)}) copy-start(bf16[256,1536]{1,0:T(8,128)(2,1)} %h_hbm.1) | copy-start | bytes 2359300
  33.4 13.2 %copy-start.1 = (f32[1536,32]{0,1:T(8,128)S(1)}, f32[1536,32]{0,1:T(8,128)}, u32[]{:S(2)}) copy-start(f32[1536,32]{0,1:T(8,128)} %param.13) | copy-start | bytes 589828
  33.4 13.2 %copy-start.2 = (s32[256,2]{0,1:T(2,128)S(1)}, s32[256,2]{0,1:T(2,128)}, u32[]{:S(2)}) copy-start(s32[256,2]{0,1:T(2,128)} %param.14) | copy-start | bytes 6148
  33.4 13.2 %copy-start.3 = (f32[2]{0:T(128)S(1)}, f32[2]{0:T(128)}, u32[]{:S(2)}) copy-start(f32[2]{0:T(128)} %param.18) | copy-start | bytes 28
